TPU v7x, 32 devices: a whole 2x2x4 slice. The times are simulated.
32 devices in a mesh: dp: 8 (over y, x, core), tp: 4 (over z).
Axes of the slice: x: 2, y: 2, z: 4, core: 2. Of those that a mesh axis runs over, the one named last changes fastest.
Arguments:
- resid: bfloat16 [2048, 4096], P('dp'), may hold values from -6 to 6
- gain: bfloat16 [4096], replicated, may hold values from 0.25 to 1.75
- grad_q: bfloat16 [2048, 3072], P('dp', 'tp'), may hold values from -1.25 to 1.25
- w_query: bfloat16 [3072, 4096], P('tp'), may hold values from -0.375 to 0.375
- grad_in: bfloat16 [2048, 4096], P('dp'), may hold values from -2 to 2
Outputs:
- weight_grad: float32 [3072, 4096], P(('tp', 'dp'))
- gain_grad: float32 [4096], replicated
- grad_out: bfloat16 [2048, 4096], P('dp')
All inputs are finite; a program needn't handle non-finite values.
Results may differ from a plain program's by a relative error of at most 0.014.
Values may be sent and summed in bfloat16 or wider, within the bound.
A program may use at most 128 MiB of HBM per device.

v0:
```python
import jax
import jax.numpy as jnp
from jax import lax
from jax.sharding import PartitionSpec as P


def norm_rows(rows_bf, gain_f):
    rows_f = rows_bf.astype(jnp.float32)
    inv_rms = lax.rsqrt(jnp.mean(rows_f * rows_f, axis=-1, keepdims=True) + 1e-05)
    unit = rows_f * inv_rms
    return (inv_rms, unit, (unit * gain_f).astype(jnp.bfloat16))


def per_device(resid, gain, grad_q, w_query, grad_in):
    gain_f = gain.astype(jnp.float32)
    inv_rms, unit, normed = norm_rows(resid, gain_f)
    local_term = jnp.dot(grad_q, w_query, preferred_element_type=jnp.float32)
    dnormed = lax.psum(local_term.astype(jnp.bfloat16), "tp").astype(jnp.float32)
    full_grad = lax.dot_general(
        grad_q, normed, (((0,), (0,)), ((), ())), preferred_element_type=jnp.float32
    )
    weight_grad = lax.psum_scatter(full_grad, "dp", scatter_dimension=0, tiled=True)
    gain_grad = lax.psum(jnp.sum(dnormed * unit, axis=0), "dp")
    dunit = dnormed * gain_f
    inner = jnp.mean(dunit * unit, axis=-1, keepdims=True)
    grad_rows = (grad_in.astype(jnp.float32) + inv_rms * (dunit - unit * inner)).astype(
        jnp.bfloat16
    )
    return (weight_grad, gain_grad, grad_rows)


def solution(mesh):
    return jax.shard_map(
        per_device,
        mesh=mesh,
        in_specs=(P("dp", None), P(), P("dp", "tp"), P("tp", None), P("dp", None)),
        out_specs=(P(("tp", "dp"), None), P(), P("dp", None)),
        check_vma=False,
    )
```

profile of v0, /device:TPU:0, one launch (start us, length us, event | category | flops | bytes accessed | tf_op | source)
XLA Modules:
  0.0 145.5 jit_solution(15786352697211024213)
XLA Ops:
  8.0 0.0 copy-start
  8.0 0.0 copy-start.2
  8.0 0.0 copy-start.1
  8.0 0.0 all-reduce.2.cloned.1.call-start
  8.1 0.9 copy-done
  9.0 5.9 %convolution_convert_fusion = bf16[256,4096]{1,0:T(8,128)(2,1)} fusion(bf16[256,768]{1,0:T(8,128)(2,1)S(1)} %copy-done, bf16[768,4096]{1,0:T(8,128)(2,1)} %param.8), kind=kOutput, calls=%fused_computation.8 | convolution fusion | flops 1611661312 | bytes 8781824 | tf_op jit(solution)/shard_map/dot_general | solution.py:17
  14.9 0.0 all-reduce.2.cloned.1.call-update
  14.9 0.0 reduce-scatter.4.cloned.1.call-start
  15.0 0.0 copy-done.2
  15.0 0.0 copy-done.1
  15.0 0.5 fusion.9
  15.5 6.6 %convolution_bitcast_fusion = f32[768,4096]{0,1:T(8,128)} fusion(bf16[256,768]{1,0:T(8,128)(2,1)S(1)} %copy-done, bf16[256,4096]{1,0:T(8,128)(2,1)S(1)} %copy-done.1, f32[4096]{0:T(1024)S(1)} %convert_element_type.22, f32[256]{0:T(256)S(1)} %add_rsqrt_fusion), kind=kOutput, calls=%fused_computation | convolution fusion | flops 1614807040 | bytes 15090688 | tf_op jit(solution)/shard_map/dot_general | solution.py:19
  22.1 12.9 %copy.10 = f32[768,4096]{1,0:T(8,128)} copy(f32[768,4096]{0,1:T(8,128)} %convolution_bitcast_fusion) | data formatting | bytes 25165824
  35.0 0.0 reduce-scatter.4.cloned.1.call-update
  35.1 68.9 %all-reduce.2.cloned.1.call-done = bf16[256,4096]{1,0:T(8,128)(2,1)} async-done(((bf16[256,4096]{1,0:T(8,128)(2,1)}), bf16[256,4096]{1,0:T(8,128)(2,1)}) %all-reduce.2.cloned.1.call-update) | async-done | bytes 2097168 | tf_op jit(solution)/shard_map/psum | solution.py:18
  103.9 3.3 %fusion.8 = (f32[256]{0:T(256)S(1)}, f32[4096]{0:T(1024)S(1)}) fusion(bf16[256,4096]{1,0:T(8,128)(2,1)S(1)} %copy-done.1, bf16[256,4096]{1,0:T(8,128)(2,1)} %all-reduce.2.cloned.1.call-done, f32[4096]{0:T(1024)S(1)} %convert_element_type.22, f32[256]{0:T(256)S(1)} %add_rsqrt_fusion), kind=kLoop, calls=%fused_computation.14 | loop fusion | flops 8384256 | bytes 4229120 | tf_op jit(solution)/shard_map/reduce_sum | solution.py:25
  107.2 25.7 %psum.15 = f32[4096]{0:T(1024)} all-reduce(f32[4096]{0:T(1024)S(1)} %get-tuple-element.10), channel_id=1, replica_groups=mesh['dp'=8,'tp'=4] {'dp'}, use_global_device_ids=true, to_apply=%region_4.0 | all-reduce | flops 4096 | bytes 32768 | tf_op jit(solution)/shard_map/psum | solution.py:23
  132.9 5.1 %fusion.6 = bf16[256,4096]{1,0:T(8,128)(2,1)} fusion(bf16[256,4096]{1,0:T(8,128)(2,1)} %all-reduce.2.cloned.1.call-done, bf16[256,4096]{1,0:T(8,128)(2,1)S(1)} %copy-done.1, bf16[256,4096]{1,0:T(8,128)(2,1)} %param.9, f32[256]{0:T(256)S(1)} %broadcast_multiply_fusion, f32[4096]{0:T(1024)S(1)} %convert_element_type.22, f32[256]{0:T(256)S(1)} %add_rsqrt_fusion), kind=kLoop, calls=%fused_computation.12 | loop fusion | flops 10485760 | bytes 8407040 | tf_op jit(solution)/shard_map/convert_element_type | solution.py:26
  138.0 0.0 reduce-scatter.4.cloned.1.call-done
  (3 shorter events, 0.0 us)
Async XLA Ops:
  8.0 1.0 copy-start
  8.0 7.0 %copy-start.2 = (bf16[4096]{0:T(1024)(128)(2,1)S(1)}, bf16[4096]{0:T(1024)(128)(2,1)}, u32[]{:S(2)}) copy-start(bf16[4096]{0:T(1024)(128)(2,1)} %param.6) | copy-start | bytes 24580
  8.0 7.0 %copy-start.1 = (bf16[256,4096]{1,0:T(8,128)(2,1)S(1)}, bf16[256,4096]{1,0:T(8,128)(2,1)}, u32[]{:S(2)}) copy-start(bf16[256,4096]{1,0:T(8,128)(2,1)} %param.5) | copy-start | bytes 6291460
  8.0 95.9 %all-reduce.2.cloned.1.call-start = ((), (), s32[]{:S(2)}) async-start(), calls=%async_computation.1 | async-start | bytes 4194304 | tf_op jit(solution)/shard_map/psum | solution.py:18
  14.9 123.1 %reduce-scatter.4.cloned.1.call-start = ((), (), s32[]{:S(2)}) async-start(), calls=%async_computation.2 | async-start | bytes 14155776
Sparse Core Ops, SparseCore 0:
  15.0 88.8 all-reduce.1
Sparse Core Ops, SparseCore 1:
  35.1 95.2 reduce-scatter.3
where the time goes:
time: 146 us; the launch traced here: 145 us
  waiting for transfers between devices  68.9 us (47%)
  blocking collectives  25.7 us (18%)
  between operations  15.5 us (11%)
  local copies, waits for them, and re-layouts  13.9 us (10%)
  matrix products  12.5 us (9%)
  other arithmetic  8.89 us (6%)
    psum x1, waiting for transfers between devices, per_device(): lax.psum(local_term.astype(jnp.bfloat16), 'tp').astype(jnp.float32)  68.9 us
    psum x1, blocking collectives, per_device(): gain_grad = lax.psum(jnp.sum(dnormed * unit, axis=0), 'dp')  25.7 us
    unnamed x7, local copies, waits for them, and re-layouts  13.9 us
    dot_general x1, matrix products, per_device(): lax.dot_general(grad_q, normed, (((0,), (0,)), ((), ())), preferred_eleme...  6.6 us
    dot_general x1, matrix products, per_device(): local_term = jnp.dot(grad_q, w_query, preferred_element_type=jnp.float32)  5.9 us
    convert_element_type x1, other arithmetic, per_device(): (grad_in.astype(jnp.float32) + inv_rms * (dunit - unit * inner)).astype(j...  5.12 us
    reduce_sum x1, other arithmetic, per_device(): inner = jnp.mean(dunit * unit, axis=-1, keepdims=True)  3.26 us
  transfers between devices with their start and end apart: 2, of which 1 were waited for; matrix products, arithmetic and copies ran while one was open for 20% of the time, Pallas kernels for 0%

commit v1 on v0

--- a/solution.py
+++ b/solution.py
@@ -20,7 +20,7 @@
         grad_q, normed, (((0,), (0,)), ((), ())), preferred_element_type=jnp.float32
     )
     weight_grad = lax.psum_scatter(full_grad, "dp", scatter_dimension=0, tiled=True)
-    gain_grad = lax.psum(jnp.sum(dnormed * unit, axis=0), "dp")
+    gain_grad = jnp.sum(lax.all_gather(jnp.sum(dnormed * unit, axis=0), "dp"), axis=0)
     dunit = dnormed * gain_f
     inner = jnp.mean(dunit * unit, axis=-1, keepdims=True)
     grad_rows = (grad_in.astype(jnp.float32) + inv_rms * (dunit - unit * inner)).astype(

time: 146 us -> 138 us (0.945)
  blocking collectives: 25.7 us -> 9.8 us
  waiting for transfers between devices: 68.9 us -> 76.5 us
    psum x1 -> x0, blocking collectives: 25.7 us -> none  [per_device(): gain_grad = lax.psum(jnp.sum(dnormed * unit, axis=0), 'dp')]
    all_gather x0 -> x1, blocking collectives: none -> 9.8 us  [per_device(): lax.all_gather(jnp.sum(dnormed * unit, axis=0), 'dp')]
    unnamed x3, waiting for transfers between devices: 0.03 us -> 7.61 us
  transfers between devices with their start and end apart: 2 -> 2, of which waited for: 1 -> 2; matrix products, arithmetic and copies ran while one was open for 20% -> 21% of each run, Pallas kernels for 0% -> 0%
where the time goes in v1:
time: 138 us
  waiting for transfers between devices  76.5 us (55%)
  between operations  15.5 us (11%)
  local copies, waits for them, and re-layouts  13.9 us (10%)
  matrix products  12.5 us (9%)
  blocking collectives  9.8 us (7%)
  other arithmetic  9.56 us (7%)
    psum x1, waiting for transfers between devices, per_device(): lax.psum(local_term.astype(jnp.bfloat16), 'tp').astype(jnp.float32)  68.9 us
    unnamed x7, local copies, waits for them, and re-layouts  13.9 us
    all_gather x1, blocking collectives, per_device(): lax.all_gather(jnp.sum(dnormed * unit, axis=0), 'dp')  9.8 us
    unnamed x3, waiting for transfers between devices  7.61 us
    dot_general x1, matrix products, per_device(): lax.dot_general(grad_q, normed, (((0,), (0,)), ((), ())), preferred_eleme...  6.6 us
    dot_general x1, matrix products, per_device(): local_term = jnp.dot(grad_q, w_query, preferred_element_type=jnp.float32)  5.9 us
    convert_element_type x1, other arithmetic, per_device(): (grad_in.astype(jnp.float32) + inv_rms * (dunit - unit * inner)).astype(j...  5.15 us
    reduce_sum x1, other arithmetic, per_device(): inner = jnp.mean(dunit * unit, axis=-1, keepdims=True)  3.26 us
  transfers between devices with their start and end apart: 2, of which 2 were waited for; matrix products, arithmetic and copies ran while one was open for 21% of the time, Pallas kernels for 0%

profile of v1, /device:TPU:0, one launch (start us, length us, event | category | flops | bytes accessed | tf_op | source)
XLA Modules:
  0.0 137.8 jit_solution(3946373238020914284)
XLA Ops:
  8.0 0.0 copy-start
  8.0 0.0 copy-start.2
  8.0 0.0 copy-start.1
  8.0 0.0 all-reduce.2.cloned.1.call-start
  8.1 0.9 copy-done
  9.0 5.9 %convolution_convert_fusion = bf16[256,4096]{1,0:T(8,128)(2,1)} fusion(bf16[256,768]{1,0:T(8,128)(2,1)S(1)} %copy-done, bf16[768,4096]{1,0:T(8,128)(2,1)} %param.8), kind=kOutput, calls=%fused_computation.8 | convolution fusion | flops 1611661312 | bytes 8781824 | tf_op jit(solution)/shard_map/dot_general | solution.py:17
  14.9 0.0 all-reduce.2.cloned.1.call-update
  14.9 0.0 reduce-scatter.4.cloned.1.call-start
  15.0 0.0 copy-done.2
  15.0 0.0 copy-done.1
  15.0 0.5 fusion.9
  15.5 6.6 %convolution_bitcast_fusion = f32[768,4096]{0,1:T(8,128)} fusion(bf16[256,768]{1,0:T(8,128)(2,1)S(1)} %copy-done, bf16[256,4096]{1,0:T(8,128)(2,1)S(1)} %copy-done.1, f32[4096]{0:T(1024)S(1)} %convert_element_type.22, f32[256]{0:T(256)S(1)} %add_rsqrt_fusion), kind=kOutput, calls=%fused_computation | convolution fusion | flops 1614807040 | bytes 15090688 | tf_op jit(solution)/shard_map/dot_general | solution.py:19
  22.1 12.9 %copy.11 = f32[768,4096]{1,0:T(8,128)} copy(f32[768,4096]{0,1:T(8,128)} %convolution_bitcast_fusion) | data formatting | bytes 25165824
  35.0 0.0 reduce-scatter.4.cloned.1.call-update
  35.1 68.9 %all-reduce.2.cloned.1.call-done = bf16[256,4096]{1,0:T(8,128)(2,1)} async-done(((bf16[256,4096]{1,0:T(8,128)(2,1)}), bf16[256,4096]{1,0:T(8,128)(2,1)}) %all-reduce.2.cloned.1.call-update) | async-done | bytes 2097168 | tf_op jit(solution)/shard_map/psum | solution.py:18
  103.9 3.3 %fusion.8 = (f32[256]{0:T(256)S(1)}, f32[4096]{0:T(1024)S(1)}) fusion(bf16[256,4096]{1,0:T(8,128)(2,1)S(1)} %copy-done.1, bf16[256,4096]{1,0:T(8,128)(2,1)} %all-reduce.2.cloned.1.call-done, f32[4096]{0:T(1024)S(1)} %convert_element_type.22, f32[256]{0:T(256)S(1)} %add_rsqrt_fusion), kind=kLoop, calls=%fused_computation.14 | loop fusion | flops 8384256 | bytes 4229120 | tf_op jit(solution)/shard_map/reduce_sum | solution.py:25
  107.2 9.8 %all-gather = f32[32768]{0:T(1024)S(1)} all-gather(f32[4096]{0:T(1024)S(1)} %get-tuple-element.13), channel_id=2, replica_groups=mesh['dp'=8,'tp'=4] {'dp'}, dimensions={0}, use_global_device_ids=true | all-gather | bytes 147456 | tf_op jit(solution)/shard_map/all_gather | solution.py:23
  117.0 0.6 reduce_sum.38
  117.7 5.2 %fusion.6 = bf16[256,4096]{1,0:T(8,128)(2,1)} fusion(bf16[256,4096]{1,0:T(8,128)(2,1)} %all-reduce.2.cloned.1.call-done, bf16[256,4096]{1,0:T(8,128)(2,1)S(1)} %copy-done.1, bf16[256,4096]{1,0:T(8,128)(2,1)} %param.9, f32[256]{0:T(256)S(1)} %broadcast_multiply_fusion, f32[4096]{0:T(1024)S(1)} %convert_element_type.22, f32[256]{0:T(256)S(1)} %add_rsqrt_fusion), kind=kLoop, calls=%fused_computation.12 | loop fusion | flops 10485760 | bytes 8407040 | tf_op jit(solution)/shard_map/convert_element_type | solution.py:26
  122.8 7.6 %reduce-scatter.4.cloned.1.call-done = f32[96,4096]{1,0:T(8,128)} async-done(((f32[768,4096]{1,0:T(8,128)}), f32[96,4096]{1,0:T(8,128)}) %reduce-scatter.4.cloned.1.call-update) | async-done | bytes 1572880
  (4 shorter events, 0.0 us)
Async XLA Ops:
  8.0 1.0 copy-start
  8.0 7.0 %copy-start.2 = (bf16[4096]{0:T(1024)(128)(2,1)S(1)}, bf16[4096]{0:T(1024)(128)(2,1)}, u32[]{:S(2)}) copy-start(bf16[4096]{0:T(1024)(128)(2,1)} %param.6) | copy-start | bytes 24580
  8.0 7.0 %copy-start.1 = (bf16[256,4096]{1,0:T(8,128)(2,1)S(1)}, bf16[256,4096]{1,0:T(8,128)(2,1)}, u32[]{:S(2)}) copy-start(bf16[256,4096]{1,0:T(8,128)(2,1)} %param.5) | copy-start | bytes 6291460
  8.0 95.9 %all-reduce.2.cloned.1.call-start = ((), (), s32[]{:S(2)}) async-start(), calls=%async_computation.1 | async-start | bytes 4194304 | tf_op jit(solution)/shard_map/psum | solution.py:18
  14.9 115.5 %reduce-scatter.4.cloned.1.call-start = ((), (), s32[]{:S(2)}) async-start(), calls=%async_computation.2 | async-start | bytes 14155776
Sparse Core Ops, SparseCore 0:
  15.0 88.8 all-reduce.1
Sparse Core Ops, SparseCore 1:
  35.1 95.2 reduce-scatter.3

commit v2 on v0

--- a/solution.py
+++ b/solution.py
@@ -15,7 +15,9 @@
     gain_f = gain.astype(jnp.float32)
     inv_rms, unit, normed = norm_rows(resid, gain_f)
     local_term = jnp.dot(grad_q, w_query, preferred_element_type=jnp.float32)
-    dnormed = lax.psum(local_term.astype(jnp.bfloat16), "tp").astype(jnp.float32)
+    dnormed = jnp.sum(lax.all_gather(local_term.astype(jnp.bfloat16), "tp"), axis=0).astype(
+        jnp.float32
+    )
     full_grad = lax.dot_general(
         grad_q, normed, (((0,), (0,)), ((), ())), preferred_element_type=jnp.float32
     )

time: 146 us -> 215 us (1.47)
  waiting for transfers between devices: 68.9 us -> 132 us
  other arithmetic: 8.89 us -> 15.8 us
    all_gather x0 -> x1, waiting for transfers between devices: none -> 132 us  [per_device(): lax.all_gather(local_term.astype(jnp.bfloat16), 'tp')]
    psum x1 -> x0, waiting for transfers between devices: 68.9 us -> none  [per_device(): lax.psum(local_term.astype(jnp.bfloat16), 'tp').astype(jnp.float32)]
    reduce_sum x0 -> x1, other arithmetic: none -> 6.89 us  [per_device(): jnp.sum(lax.all_gather(local_term.astype(jnp.bfloat16), 'tp'), axis=0)]
  transfers between devices with their start and end apart: 2 -> 2, of which waited for: 1 -> 1; matrix products, arithmetic and copies ran while one was open for 20% -> 16% of each run, Pallas kernels for 0% -> 0%
where the time goes in v2:
time: 215 us
  waiting for transfers between devices  132 us (61%)
  blocking collectives  24.7 us (11%)
  other arithmetic  15.8 us (7%)
  between operations  15.5 us (7%)
  local copies, waits for them, and re-layouts  13.9 us (6%)
  matrix products  12.5 us (6%)
    all_gather x1, waiting for transfers between devices, per_device(): lax.all_gather(local_term.astype(jnp.bfloat16), 'tp')  132 us
    psum x1, blocking collectives, per_device(): gain_grad = lax.psum(jnp.sum(dnormed * unit, axis=0), 'dp')  24.7 us
    unnamed x7, local copies, waits for them, and re-layouts  13.9 us
    reduce_sum x1, other arithmetic, per_device(): jnp.sum(lax.all_gather(local_term.astype(jnp.bfloat16), 'tp'), axis=0)  6.89 us
    dot_general x1, matrix products, per_device(): lax.dot_general(grad_q, normed, (((0,), (0,)), ((), ())), preferred_eleme...  6.58 us
    dot_general x1, matrix products, per_device(): local_term = jnp.dot(grad_q, w_query, preferred_element_type=jnp.float32)  5.9 us
    convert_element_type x1, other arithmetic, per_device(): (grad_in.astype(jnp.float32) + inv_rms * (dunit - unit * inner)).astype(j...  5.15 us
  transfers between devices with their start and end apart: 2, of which 1 were waited for; matrix products, arithmetic and copies ran while one was open for 16% of the time, Pallas kernels for 0%

profile of v2, /device:TPU:0, one launch (start us, length us, event | category | flops | bytes accessed | tf_op | source)
XLA Modules:
  0.0 214.9 jit_solution(2445045716249100223)
XLA Ops:
  8.0 0.0 copy-start
  8.0 0.0 copy-start.2
  8.0 0.0 copy-start.1
  8.0 0.0 all-gather.3.cloned.1.call-start
  8.1 0.9 copy-done
  9.0 5.9 %convolution_convert_fusion = bf16[256,4096]{1,0:T(8,128)(2,1)} fusion(bf16[256,768]{1,0:T(8,128)(2,1)S(1)} %copy-done, bf16[768,4096]{1,0:T(8,128)(2,1)} %param.8), kind=kOutput, calls=%fused_computation.8 | convolution fusion | flops 1611661312 | bytes 8781824 | tf_op jit(solution)/shard_map/dot_general | solution.py:17
  14.9 0.0 all-gather.3.cloned.1.call-update
  14.9 0.0 reduce-scatter.4.cloned.1.call-start
  15.0 0.0 copy-done.2
  15.0 0.0 copy-done.1
  15.0 0.5 fusion.9
  15.5 6.6 %convolution_bitcast_fusion = f32[768,4096]{0,1:T(8,128)} fusion(bf16[256,768]{1,0:T(8,128)(2,1)S(1)} %copy-done, bf16[256,4096]{1,0:T(8,128)(2,1)S(1)} %copy-done.1, f32[4096]{0:T(1024)S(1)} %convert_element_type.24, f32[256]{0:T(256)S(1)} %add_rsqrt_fusion), kind=kOutput, calls=%fused_computation | convolution fusion | flops 1614807040 | bytes 15090688 | tf_op jit(solution)/shard_map/dot_general | solution.py:21
  22.1 12.9 %copy.10 = f32[768,4096]{1,0:T(8,128)} copy(f32[768,4096]{0,1:T(8,128)} %convolution_bitcast_fusion) | data formatting | bytes 25165824
  35.0 0.0 reduce-scatter.4.cloned.1.call-update
  35.0 132.4 %all-gather.3.cloned.1.call-done = bf16[1024,4096]{1,0:T(8,128)(2,1)} async-done(((bf16[256,4096]{1,0:T(8,128)(2,1)}), bf16[1024,4096]{1,0:T(8,128)(2,1)}) %all-gather.3.cloned.1.call-update) | async-done | bytes 8388624 | tf_op jit(solution)/shard_map/all_gather | solution.py:18
  167.4 6.9 %reduce_sum.40 = bf16[256,4096]{1,0:T(8,128)(2,1)} reduce(bf16[4,256,4096]{2,1,0:T(8,128)(2,1)} %bitcast.7, bf16[]{:T(256)} %constant.9.clone.1), dimensions={0}, to_apply=%region_2.0 | reduce | flops 3145728 | bytes 10485762 | tf_op jit(solution)/shard_map/reduce_sum | solution.py:18
  174.3 3.3 %fusion.8 = (f32[256]{0:T(256)S(1)}, f32[4096]{0:T(1024)S(1)}) fusion(bf16[256,4096]{1,0:T(8,128)(2,1)S(1)} %copy-done.1, bf16[256,4096]{1,0:T(8,128)(2,1)} %reduce_sum.40, f32[4096]{0:T(1024)S(1)} %convert_element_type.24, f32[256]{0:T(256)S(1)} %add_rsqrt_fusion), kind=kLoop, calls=%fused_computation.14 | loop fusion | flops 8384256 | bytes 4229120 | tf_op jit(solution)/shard_map/reduce_sum | solution.py:27
  177.6 24.7 %psum.7 = f32[4096]{0:T(1024)} all-reduce(f32[4096]{0:T(1024)S(1)} %get-tuple-element.10), channel_id=1, replica_groups=mesh['dp'=8,'tp'=4] {'dp'}, use_global_device_ids=true, to_apply=%region_4.0 | all-reduce | flops 4096 | bytes 32768 | tf_op jit(solution)/shard_map/psum | solution.py:25
  202.3 5.2 %fusion.6 = bf16[256,4096]{1,0:T(8,128)(2,1)} fusion(bf16[256,4096]{1,0:T(8,128)(2,1)} %reduce_sum.40, bf16[256,4096]{1,0:T(8,128)(2,1)S(1)} %copy-done.1, bf16[256,4096]{1,0:T(8,128)(2,1)} %param.9, f32[256]{0:T(256)S(1)} %broadcast_multiply_fusion, f32[4096]{0:T(1024)S(1)} %convert_element_type.24, f32[256]{0:T(256)S(1)} %add_rsqrt_fusion), kind=kLoop, calls=%fused_computation.12 | loop fusion | flops 10485760 | bytes 8407040 | tf_op jit(solution)/shard_map/convert_element_type | solution.py:28
  207.5 0.0 reduce-scatter.4.cloned.1.call-done
  (3 shorter events, 0.0 us)
Async XLA Ops:
  8.0 1.0 copy-start
  8.0 7.0 %copy-start.2 = (bf16[4096]{0:T(1024)(128)(2,1)S(1)}, bf16[4096]{0:T(1024)(128)(2,1)}, u32[]{:S(2)}) copy-start(bf16[4096]{0:T(1024)(128)(2,1)} %param.6) | copy-start | bytes 24580
  8.0 7.0 %copy-start.1 = (bf16[256,4096]{1,0:T(8,128)(2,1)S(1)}, bf16[256,4096]{1,0:T(8,128)(2,1)}, u32[]{:S(2)}) copy-start(bf16[256,4096]{1,0:T(8,128)(2,1)} %param.5) | copy-start | bytes 6291460
  8.0 159.4 %all-gather.3.cloned.1.call-start = ((), (), s32[]{:S(2)}) async-start(), calls=%async_computation.1 | async-start | bytes 10485760 | tf_op jit(solution)/shard_map/all_gather | solution.py:18
  14.9 192.5 %reduce-scatter.4.cloned.1.call-start = ((), (), s32[]{:S(2)}) async-start(), calls=%async_computation.2 | async-start | bytes 14155776
Sparse Core Ops, SparseCore 0:
  15.0 152.3 all-gather.2
Sparse Core Ops, SparseCore 1:
  35.1 95.0 reduce-scatter.3
